TPU v7x, 32 devices: a 4x4x1 block of a 4x4x8 slice. The times are simulated.
32 devices in a mesh: dp: 1 (over z), sp: 32 (over x, y, core).
Axes of the slice: x: 4, y: 4, z: 1, core: 2. Of those that a mesh axis runs over, the one named last changes fastest.
The devices are a block of a 4x4x8 slice.
Arguments:
- q: bfloat16 [32, 56, 128], P('dp')
- k: bfloat16 [32, 4096, 56, 128], P('dp', 'sp')
- v: bfloat16 [32, 4096, 56, 128], P('dp', 'sp')
Outputs:
- q: bfloat16 [32, 56, 128], P('dp')
All inputs are finite; a program needn't handle non-finite values.
Results may differ from a plain program's by a relative error of at most 0.012.
Values are sent between devices in bfloat16 or wider.
A program may use at most 768 MiB of HBM per device.

v0:
```python
import jax
import jax.numpy as jnp
from jax import lax
from jax.sharding import PartitionSpec as P


def einsum(form, a, b):
    return jnp.einsum(form, a.astype(jnp.float32), b.astype(jnp.float32))


def part_of(q, k, v):
    grouped = q.reshape(q.shape[0], k.shape[2], -1, q.shape[2])
    scores = einsum("bgsd,bugd->bgsu", grouped, k) * q.shape[2] ** -0.5
    high = jnp.max(scores, -1, keepdims=True)
    weights = jnp.exp(scores - high)
    seen = einsum("bgsu,bugd->bgsd", weights.astype(jnp.bfloat16), v)
    return jnp.concatenate([seen, jnp.sum(weights, -1, keepdims=True), high], -1)


def together(parts):
    seen, total, high = parts[..., :-2], parts[..., -2:-1], parts[..., -1:]
    scale = jnp.exp(high - jnp.max(high, 0))
    return (jnp.sum(seen * scale, 0) / jnp.sum(total * scale, 0)).astype(jnp.bfloat16)


def solution(mesh):
    def step(q, k, v):
        return together(lax.all_gather(part_of(q, k, v), "sp")).reshape(q.shape)

    return jax.shard_map(
        step,
        mesh=mesh,
        in_specs=(P("dp", None, None), P("dp", "sp", None, None), P("dp", "sp", None, None)),
        out_specs=P("dp", None, None),
        check_vma=False,
    )
```

profile of v0, /device:TPU:97, one launch (start us, length us, event | category | flops | bytes accessed | tf_op | source)
XLA Modules:
  0.0 307.3 jit_solution(1409849041001496627)
XLA Ops:
  6.5 0.0 all-gather.3.cloned.1.call-start
  6.6 38.3 %fusion.3 = f32[32,56,1,128]{3,2,1,0:T(1,128)S(1)} fusion(bf16[32,128,56,128]{3,2,1,0:T(8,128)(2,1)} %param.4, bf16[32,56,128,1]{2,1,0,3:T(8,128)(2,1)} %bitcast.15), kind=kOutput, calls=%fused_computation.4 | convolution fusion | flops 58720256 | bytes 60096512 | tf_op jit(solution)/shard_map/bgsd,bugd->bgsu/dot_general | solution.py:8
  44.9 0.3 multiply_reduce_fusion
  45.2 0.6 fusion.10
  45.8 22.6 %fusion.1 = f32[32,56,1,128]{3,2,1,0:T(1,128)S(1)} fusion(bf16[32,128,56,128]{3,2,1,0:T(8,128)(2,1)} %param.5, bf16[32,56,128,1]{2,1,0,3:T(8,128)(2,1)S(1)} %get-tuple-element.7), kind=kOutput, calls=%fused_computation.2 | convolution fusion | flops 58720256 | bytes 60096512 | tf_op jit(solution)/shard_map/bgsu,bugd->bgsd/dot_general | solution.py:8
  68.4 1.2 copy.12
  69.6 1.6 pad_maximum_fusion
  71.2 0.1 all-gather.3.cloned.1.call-update
  71.3 203.0 %all-gather.3.cloned.1.call-done = f32[1024,56,1,130]{1,0,3,2:T(8,128)} async-done(((f32[32,56,1,130]{1,0,3,2:T(8,128)}), f32[1024,56,1,130]{1,0,3,2:T(8,128)}) %all-gather.3.cloned.1.call-update) | async-done | bytes 29818896 | tf_op jit(solution)/shard_map/all_gather | solution.py:28
  274.3 1.1 slice_reduce_fusion
  275.4 1.3 fusion.9
  276.7 21.6 %fusion = f32[32,56,128]{1,0,2:T(8,128)S(1)} fusion(f32[32,32,56,1,130]{2,1,0,4,3:T(8,128)} %bitcast.7, f32[32,32,56]{2,1,0:T(8,128)S(1)} %get-tuple-element.6), kind=kLoop, calls=%fused_computation.1 | loop fusion | flops 14450688 | bytes 30507008 | tf_op jit(solution)/shard_map/reduce_sum | solution.py:23
  298.3 0.2 divide_convert_fusion
  298.6 1.8 copy.6
Async XLA Ops:
  6.5 267.8 %all-gather.3.cloned.1.call-start = ((), (), s32[]{:S(2)}) async-start(), calls=%async_computation | async-start | bytes 70287360 | tf_op jit(solution)/shard_map/all_gather | solution.py:28
Sparse Core Ops, SparseCore 0:
  71.4 202.8 all-gather.2
where the time goes:
time: 307 us
  waiting for transfers between devices  203 us (66%)
  matrix products  60.9 us (20%)
  other arithmetic  26.8 us (9%)
  between operations  13.4 us (4%)
    all_gather x1, waiting for transfers between devices, step(): return together(lax.all_gather(part_of(q, k, v), 'sp')).reshape(q.shape)  203 us
    dot_general x2, matrix products, einsum(): return jnp.einsum(form, a.astype(jnp.float32), b.astype(jnp.float32))  60.9 us
    reduce_sum x1, other arithmetic, together(): jnp.sum(seen * scale, 0) / jnp.sum(total * scale, 0)  21.6 us
  transfers between devices with their start and end apart: 1, of which 1 were waited for; matrix products, arithmetic and copies ran while one was open for 0% of the time, Pallas kernels for 0%

commit v1 on v0

v1 whole, which is shorter than its diff:
```python
import functools
import math

import jax
import jax.numpy as jnp
from jax import lax
from jax.experimental import pallas as pl
from jax.experimental.pallas import tpu as pltpu
from jax.sharding import PartitionSpec as P

MESH = pl.DeviceIdType.MESH
GROUP = 4
RING = 14
LAG = 5
TILE = 16
LANES = 256


def kernel(n, heads, scale, q_ref, k_ref, v_ref, out_ref, ring, qbuf, scores, pick, spread, stat, stats, high, share, parts, inbox, mine, ring_sem, q_sem, stat_send, stat_recv, part_send, part_recv, out_send, out_recv):
    me = lax.axis_index("sp")
    pairs, rows, head = k_ref.shape[0], k_ref.shape[2], k_ref.shape[3]
    width = pick.shape[1]
    chunks = rows // width
    both = 2 * heads
    per_pair = both // TILE
    blocks = pairs * per_pair

    def item(t):
        slot = lax.rem(t, RING)
        return ring.at[slot], ring_sem.at[slot]

    def fetch(t):
        dst, sem = item(t)

        @pl.when(t < pairs)
        def _():
            pltpu.make_async_copy(k_ref.at[t], dst, sem).start()

        @pl.when(jnp.logical_and(t >= pairs, t < 2 * pairs))
        def _():
            pltpu.make_async_copy(v_ref.at[t - pairs], dst, sem).start()

    def arrived(t):
        dst, sem = item(t)
        pltpu.make_async_copy(k_ref.at[0], dst, sem).wait()

    def peers(act):
        def one(s, _):
            act(lax.rem(me + s, n))
            return 0

        lax.fori_loop(1, n, one, 0)

    load_q = pltpu.make_async_copy(q_ref, qbuf, q_sem)
    load_q.start()
    for t in range(RING):
        fetch(jnp.int32(t))
    barrier = pltpu.get_barrier_semaphore()
    peers(lambda peer: pl.semaphore_signal(barrier, inc=1, device_id={"sp": peer}, device_id_type=MESH))

    column_head = lax.rem(lax.broadcasted_iota(jnp.int32, (TILE, width), 1), heads)
    row = lax.broadcasted_iota(jnp.int32, (TILE, width), 0)
    for r in range(0, heads, 8):
        pick[r : r + 8, :] = jnp.where(column_head[:8] == row[:8] + r, 1.0, 0.0)
    entries = [(i, b) for i in range(per_pair) for b in range(2) if i * TILE < (b + 1) * heads and (i + 1) * TILE > b * heads]
    for e, (i, b) in enumerate(entries):
        spread[e] = jnp.where(column_head == row + (i * TILE - b * heads), 1.0, 0.0).astype(jnp.bfloat16)
    stat[...] = jnp.zeros_like(stat)

    def fold(x, op):
        shift = width // 2
        while shift >= heads:
            x = op(x, pltpu.roll(x, shift, 1))
            shift //= 2
        return x

    def per_sequence(x, reduce):
        return [reduce(x[b * chunks : (b + 1) * chunks], 0, keepdims=True) for b in range(2)]

    def over_chunks(two):
        return jnp.concatenate([jnp.broadcast_to(x, (chunks, width)) for x in two], 0)

    def score(p):
        kv, _ = item(p)
        qp = qbuf[p].astype(jnp.float32)
        first = lax.broadcasted_iota(jnp.int32, (both, head), 0) < heads
        qq = jnp.concatenate([jnp.where(first, qp, 0.0), jnp.where(first, 0.0, qp)], 1).astype(jnp.bfloat16)
        for c in range(chunks):
            for j in range(width // LANES):
                at = pl.ds(c * width + j * LANES, LANES)
                cols = slice(j * LANES, (j + 1) * LANES)
                kk = jnp.concatenate([kv[0, at, :], kv[1, at, :]], 1)
                s = lax.dot_general(qq, kk, (((1,), (1,)), ((), ())), preferred_element_type=jnp.float32)
                wanted = pick[:, cols] != 0.0
                for b in range(2):
                    own = jnp.where(wanted, s[b * heads : (b + 1) * heads], 0.0)
                    scores[p, b * chunks + c : b * chunks + c + 1, cols] = jnp.sum(own, 0, keepdims=True)

    lane = lax.broadcasted_iota(jnp.int32, (1, 128), 1)
    tile_row = lax.broadcasted_iota(jnp.int32, (8, 128), 0)

    def local_stats(p):
        s = scores[p] * scale
        top = per_sequence(fold(s, jnp.maximum), jnp.max)
        total = per_sequence(fold(jnp.exp(s - over_chunks(top)), jnp.add), jnp.sum)
        at = lax.rem(p, GROUP)
        old = stat[...]
        for two, first in ((top, 0), (total, GROUP)):
            line = jnp.where(lane < heads, two[0][:, :128], two[1][:, :128])
            old = jnp.where(tile_row == at + first, jnp.broadcast_to(line, (8, 128)), old)
        stat[...] = old

    def send_stats(g):
        stats[g, me] = stat[...]
        peers(
            lambda peer: pltpu.make_async_remote_copy(
                stats.at[g, me], stats.at[g, me], stat_send.at[g], stat_recv.at[g], device_id={"sp": peer}, device_id_type=MESH
            ).start()
        )

    def all_stats(g):
        some = stats.at[g, pl.ds(0, n - 1)]
        pltpu.make_async_copy(some, some, stat_recv.at[g]).wait()
        x = stats[g]
        top = jnp.max(x, 0, keepdims=True)
        scaled = jnp.exp(pltpu.roll(x - top, GROUP, 1)) * x
        total = jnp.sum(scaled, 0)
        for ref, four in ((high, top[0, :GROUP]), (share, 1.0 / total[GROUP:])):
            lanes = lax.broadcasted_iota(jnp.int32, (GROUP, 128), 1)
            eight = jnp.concatenate([jnp.where(lanes < heads, four, 0.0), jnp.where(jnp.logical_and(lanes >= heads, lanes < both), four, 0.0)], 0)
            wide = jnp.concatenate([eight, jnp.zeros((2 * GROUP, width - 128), jnp.float32)], 1)
            shift = heads
            while shift < width:
                wide = wide + pltpu.roll(wide, shift, 1)
                shift *= 2
            for i in range(GROUP):
                ref[i] = over_chunks([wide[i : i + 1], wide[GROUP + i : GROUP + i + 1]])

    def attend(p):
        kv, _ = item(p + pairs)
        at = lax.rem(p, GROUP)
        w = jnp.exp(scores[p] * scale - high[at]) * share[at]
        acc = jnp.zeros((both, 2 * head), jnp.float32)
        for c in range(chunks):
            lines = [jnp.broadcast_to(w[b * chunks + c : b * chunks + c + 1], (TILE, width)).astype(jnp.bfloat16) for b in range(2)]
            lhs = [None] * per_pair
            for e, (i, b) in enumerate(entries):
                term = lines[b] * spread[e]
                lhs[i] = term if lhs[i] is None else lhs[i] + term
            vv = jnp.concatenate([kv[0, c * width : (c + 1) * width, :], kv[1, c * width : (c + 1) * width, :]], 1)
            acc = acc + jnp.dot(jnp.concatenate(lhs, 0), vv, preferred_element_type=jnp.float32)
        part = jnp.concatenate([acc[:heads, :head], acc[heads:, head:]], 0).astype(jnp.bfloat16)
        for i in range(per_pair):
            parts[p * per_pair + i] = part[i * TILE : (i + 1) * TILE]

    def part_copy(b):
        return pltpu.make_async_remote_copy(
            parts.at[b], inbox.at[b // n, me], part_send.at[b], part_recv.at[b // n], device_id={"sp": lax.rem(b, n)}, device_id_type=MESH
        )

    def send_parts(p):
        def one(i, _):
            b = p * per_pair + i

            @pl.when(lax.rem(b, n) == me)
            def _():
                inbox[b // n, me] = parts[b]

            @pl.when(lax.rem(b, n) != me)
            def _():
                part_copy(b).start()

            return 0

        lax.fori_loop(0, per_pair, one, 0)

    def add_up(p):
        i = lax.rem(me + n * blocks - p * per_pair, n)

        @pl.when(i < per_pair)
        def _():
            b = p * per_pair + i
            j = b // n
            some = inbox.at[j, pl.ds(0, n - 1)]
            pltpu.make_async_copy(some, some, part_recv.at[j]).wait()
            mine[j] = jnp.sum(inbox[j].astype(jnp.float32), 0).astype(jnp.bfloat16)
            pltpu.make_async_copy(mine.at[j], out_ref.at[b], out_recv).start()
            peers(
                lambda peer: pltpu.make_async_remote_copy(
                    mine.at[j], out_ref.at[b], out_send.at[j], out_recv, device_id={"sp": peer}, device_id_type=MESH
                ).start()
            )

    load_q.wait()
    arrived(jnp.int32(0))
    score(0)
    fetch(jnp.int32(RING))
    pl.semaphore_wait(barrier, n - 1)

    def key_step(p, _):
        arrived(p)
        local_stats(p - 1)
        score(p)
        fetch(p + RING)

        @pl.when(lax.rem(p, GROUP) == 0)
        def _():
            send_stats(p // GROUP - 1)

        return 0

    lax.fori_loop(1, pairs, key_step, 0)
    local_stats(pairs - 1)
    send_stats(pairs // GROUP - 1)

    def value_step(p, _):
        @pl.when(lax.rem(p, GROUP) == 0)
        def _():
            all_stats(p // GROUP)

        arrived(p + pairs)
        attend(p)
        fetch(p + pairs + RING)
        send_parts(p)

        @pl.when(p >= LAG)
        def _():
            add_up(p - LAG)

        return 0

    lax.fori_loop(0, pairs, value_step, 0)

    def drain(p, _):
        add_up(p)
        return 0

    lax.fori_loop(pairs - LAG, pairs, drain, 0)

    for g in range(pairs // GROUP):
        some = stats.at[g, pl.ds(0, n - 1)]
        pltpu.make_async_copy(some, some, stat_send.at[g]).wait()

    def sent(b, _):
        @pl.when(lax.rem(b, n) != me)
        def _():
            part_copy(b).wait_send()

        return 0

    lax.fori_loop(0, blocks, sent, 0)
    for j in range(mine.shape[0]):

        @pl.when(j * n + me < blocks)
        def _():
            some = inbox.at[j, pl.ds(0, n - 1)]
            pltpu.make_async_copy(some, some, out_send.at[j]).wait()

    pltpu.make_async_copy(out_ref, out_ref, out_recv).wait()


def solution(mesh):
    n = mesh.shape["sp"]

    def step(q, k, v):
        batch, heads, head = q.shape
        tokens = k.shape[1]
        pairs, rows = batch // 2, tokens * heads
        width = math.lcm(heads, LANES)
        chunks = rows // width
        per_pair = 2 * heads // TILE
        blocks = pairs * per_pair
        owned = -(-blocks // n)
        groups = pairs // GROUP
        entries = per_pair + (heads % TILE != 0)
        f32, bf16 = jnp.float32, jnp.bfloat16
        out = pl.pallas_call(
            functools.partial(kernel, n, heads, head**-0.5),
            out_shape=jax.ShapeDtypeStruct((blocks, TILE, head), bf16),
            in_specs=[pl.BlockSpec(memory_space=pl.ANY)] * 3,
            out_specs=pl.BlockSpec(memory_space=pl.ANY),
            scratch_shapes=[
                pltpu.VMEM((RING, 2, rows, head), bf16),
                pltpu.VMEM((pairs, 2 * heads, head), bf16),
                pltpu.VMEM((pairs, 2 * chunks, width), f32),
                pltpu.VMEM((heads, width), f32),
                pltpu.VMEM((entries, TILE, width), bf16),
                pltpu.VMEM((2 * GROUP, 128), f32),
                pltpu.VMEM((groups, n, 2 * GROUP, 128), f32),
                pltpu.VMEM((GROUP, 2 * chunks, width), f32),
                pltpu.VMEM((GROUP, 2 * chunks, width), f32),
                pltpu.VMEM((blocks, TILE, head), bf16),
                pltpu.VMEM((owned, n, TILE, head), bf16),
                pltpu.VMEM((owned, TILE, head), bf16),
                pltpu.SemaphoreType.DMA((RING,)),
                pltpu.SemaphoreType.DMA,
                pltpu.SemaphoreType.DMA((groups,)),
                pltpu.SemaphoreType.DMA((groups,)),
                pltpu.SemaphoreType.DMA((blocks,)),
                pltpu.SemaphoreType.DMA((owned,)),
                pltpu.SemaphoreType.DMA((owned,)),
                pltpu.SemaphoreType.DMA,
            ],
            compiler_params=pltpu.CompilerParams(collective_id=0, has_side_effects=True, vmem_limit_bytes=66 * 1000 * 1000),
            cost_estimate=pl.CostEstimate(flops=8 * batch * rows * head, bytes_accessed=4 * batch * rows * head, transcendentals=2 * batch * rows),
            name="attend",
        )(q.reshape(pairs, 2 * heads, head), k.reshape(pairs, 2, rows, head), v.reshape(pairs, 2, rows, head))
        return out.reshape(q.shape)

    return jax.shard_map(
        step,
        mesh=mesh,
        in_specs=(P("dp", None, None), P("dp", "sp", None, None), P("dp", "sp", None, None)),
        out_specs=P("dp", None, None),
        check_vma=False,
    )
```

time: 307 us -> 75.6 us (0.25)
  waiting for transfers between devices: 203 us -> 0 us
  Pallas kernels: 0 us -> 73.6 us
  matrix products: 60.9 us -> 0 us
  other arithmetic: 26.8 us -> 0 us
  between operations: 13.4 us -> 0.01 us
    all_gather x1 -> x0, waiting for transfers between devices: 203 us -> none  [step(): return together(lax.all_gather(part_of(q, k, v), 'sp')).reshape(q.shape)]
    pallas_call x0 -> x1, Pallas kernels: none -> 73.6 us  [step(): pl.pallas_call(functools.partial(kernel, n, heads, head ** (-0.5)), out_s...]
    dot_general x2 -> x0, matrix products: 60.9 us -> none  [einsum(): return jnp.einsum(form, a.astype(jnp.float32), b.astype(jnp.float32))]
    reduce_sum x2 -> x0, other arithmetic: 22.9 us -> none  [the longest x1 21.6 us: together(): jnp.sum(seen * scale, 0) / jnp.sum(total * scale, 0)]
  transfers between devices with their start and end apart: 1 -> 0, of which waited for: 1 -> 0; matrix products, arithmetic and copies ran while one was open for 0% -> 0% of each run, Pallas kernels for 0% -> 0%
where the time goes in v1:
time: 75.6 us; the launch traced here: 75.5 us
  Pallas kernels  73.6 us (97%)
  local copies, waits for them, and re-layouts  1.82 us (2%)
    pallas_call x1, Pallas kernels, step(): pl.pallas_call(functools.partial(kernel, n, heads, head ** (-0.5)), out_s...  73.6 us
    unnamed x1, local copies, waits for them, and re-layouts  1.82 us

profile of v1, /device:TPU:97, one launch (start us, length us, event | category | flops | bytes accessed | tf_op | source)
XLA Modules:
  0.0 75.5 jit_solution(5211927819325589520)
XLA Ops:
  0.0 73.6 %attend.1 = bf16[112,16,128]{2,1,0:T(8,128)(2,1)} custom-call(bf16[16,112,128]{2,1,0:T(8,128)(2,1)} %bitcast.7, bf16[16,2,7168,128]{3,2,1,0:T(8,128)(2,1)} %bitcast.4, bf16[16,2,7168,128]{3,2,1,0:T(8,128)(2,1)} %bitcast.5), custom_call_target="tpu_custom_call" | custom-call | flops 234881024 | bytes 117440512 | tf_op jit(solution)/shard_map/attend/pallas_call | solution.py:277
  73.6 1.8 %copy.5 = bf16[32,56,128]{2,1,0:T(8,128)(2,1)} copy(bf16[32,56,128]{2,1,0:T(8,128)(2,1)} %bitcast.6) | data formatting | bytes 917504
